TPU v7x, 256 devices: a whole 4x4x8 slice. The times are simulated.
256 devices in a mesh: mem: 16 (over z, core), ma: 16 (over x, y).
Axes of the slice: x: 4, y: 4, z: 8, core: 2. Of those that a mesh axis runs over, the one named last changes fastest.
Arguments:
- ar_state: float32 [3, 64, 128, 2, 1280], P(None, 'mem', 'ma'), may hold values from -4 to 4
- forcing: float32 [3, 64, 128, 2, 1280], P(None, 'mem', 'ma'), may hold values from -6 to 6
- ar_decay: float32 [3], replicated, may hold values from 0.3 to 0.95
- amplitude: float32 [3, 1280], replicated, may hold values from 0.05 to 0.4
- wavenumber: int32 [128], replicated, may hold values from 0 to 1279, as said below
- tables: bfloat16 [128, 1280, 1280], P('ma', None, 'mem'), may hold values from -0.15625 to 0.15625
- tendencies: bfloat16 [64, 1280, 5120], P('mem', 'ma'), may hold values from -6 to 6
Outputs:
- perturbed: bfloat16 [64, 1280, 5120], P('mem', 'ma')
- new_state: float32 [3, 64, 128, 2, 1280], P(None, 'mem', 'ma')
Inputs may be any that keep to these rules, and one draw needn't show every extreme that they name: `wavenumber`: 128 distinct values.
All inputs are finite; a program needn't handle non-finite values.
Results may differ from a plain program's by a relative error of at most 0.0042.
Values may be sent and summed in bfloat16 or wider, within the bound.
No kernel may reach another device: no remote copies, remote signals or barrier semaphores. Data moves between devices by JAX's collectives and lax.ppermute only.
A program may use at most 64 MiB of HBM per device.

v0:
```python
import math
import jax
import jax.numpy as jnp
from jax import lax
from jax.sharding import PartitionSpec as P

clip_level = 0.9


def basis_table(wavenumber, lon_count):
    longitude = lax.broadcasted_iota(jnp.int32, (wavenumber.shape[0], lon_count), 1)
    phases = wavenumber[:, None] * longitude % lon_count
    angles = phases.astype(jnp.float32) * (2.0 * math.pi / lon_count)
    stacked = jnp.stack([jnp.cos(angles), -jnp.sin(angles)], axis=1)
    return stacked.reshape(2 * wavenumber.shape[0], lon_count).astype(jnp.bfloat16)


def per_device(ar_state, forcing, ar_decay, amplitude, wavenumber, tables, tendencies):
    local_waves = ar_state.shape[2]
    degree_count = ar_state.shape[4]
    owner_index = lax.axis_index("ma")
    own_waves = lax.dynamic_slice_in_dim(wavenumber, owner_index * local_waves, local_waves)
    degree_grid = lax.broadcasted_iota(jnp.int32, (local_waves, degree_count), 1)
    kept_mask = (degree_grid >= own_waves[:, None]).astype(jnp.float32)
    updated = (
        ar_decay[:, None, None, None, None] * ar_state + amplitude[:, None, None, None, :] * forcing
    )
    new_state = kept_mask[None, None, :, None, :] * updated
    coefficients = jnp.sum(new_state, axis=0).astype(jnp.bfloat16)
    everyone = lax.all_gather(coefficients, "mem", axis=0, tiled=True)
    product = jnp.einsum("bmcn,mnl->blmc", everyone, tables, preferred_element_type=jnp.float32)
    fourier = product.astype(jnp.bfloat16)
    banded = lax.all_to_all(
        lax.all_to_all(fourier, "mem", split_axis=0, concat_axis=1, tiled=True),
        "ma",
        split_axis=1,
        concat_axis=2,
        tiled=True,
    )
    member_count, lat_rows, window_size, reim_parts = banded.shape
    basis = basis_table(wavenumber, tendencies.shape[2])
    fourier_rows = banded.reshape(member_count * lat_rows, window_size * reim_parts)
    pattern = jnp.dot(fourier_rows, basis, preferred_element_type=jnp.float32) * (
        1.0 / math.sqrt(window_size)
    )
    pattern = jnp.clip(pattern, -clip_level, clip_level).reshape(tendencies.shape)
    perturbed = (tendencies.astype(jnp.float32) * (1.0 + pattern)).astype(jnp.bfloat16)
    return (perturbed, new_state)


def solution(mesh):
    return jax.shard_map(
        per_device,
        mesh=mesh,
        in_specs=(
            P(None, "mem", "ma", None, None),
            P(None, "mem", "ma", None, None),
            P(),
            P(),
            P(),
            P("ma", None, "mem"),
            P("mem", "ma", None),
        ),
        out_specs=(P("mem", "ma", None), P(None, "mem", "ma", None, None)),
        check_vma=False,
    )
```

profile of v0, /device:TPU:1, one launch (start us, length us, event | category | flops | bytes accessed | tf_op | source)
XLA Modules:
  0.0 131.1 jit_solution(6090136942241296516)
XLA Ops:
  7.2 0.0 copy-start
  7.2 0.0 all-gather.2.cloned.1.call-start
  7.2 0.8 dynamic_slice.3
  8.1 0.1 fusion.20
  8.1 3.5 %fusion.21 = (bf16[4,8,2,1280]{3,2,1,0:T(2,128)(2,1)S(1)}, f32[3,4,8,2,1280]{4,3,2,1,0:T(2,128)}) fusion(f32[3,4,8,2,1280]{4,3,2,1,0:T(2,128)} %param.8, f32[3,1280]{1,0:T(4,128)} %param.10, f32[3,4,8,2,1280]{4,3,2,1,0:T(2,128)} %param.7, f32[3]{0:T(128)} %param.9, f32[8,1280]{1,0:T(8,128)S(1)} %fusion.20), kind=kLoop, calls=%fused_computation.23 | loop fusion | flops 1146880 | bytes 3169292 | tf_op jit(solution)/shard_map/reduce_sum | solution.py:29
  11.6 0.7 copy.23
  12.3 0.0 all-gather.2.cloned.1.call-update
  12.3 0.0 copy-start.2
  12.3 44.4 %all-gather.2.cloned.1.call-done = bf16[64,8,2,1280]{3,1,2,0:T(8,128)(2,1)} async-done(((bf16[4,8,2,1280]{3,1,2,0:T(8,128)(2,1)}), bf16[64,8,2,1280]{3,1,2,0:T(8,128)(2,1)}) %all-gather.2.cloned.1.call-update) | async-done | bytes 2621456 | tf_op jit(solution)/shard_map/all_gather | solution.py:30
  56.7 0.0 copy-done
  56.7 2.7 %fusion.15 = bf16[64,80,8,2]{1,0,3,2:T(8,128)(2,1)S(1)} fusion(bf16[8,1280,80]{1,2,0:T(8,128)(2,1)S(1)} %copy-done, bf16[64,8,2,1280]{3,1,2,0:T(8,128)(2,1)} %all-gather.2.cloned.1.call-done), kind=kOutput, calls=%fused_computation.18 | convolution fusion | flops 209797120 | bytes 4423680 | tf_op jit(solution)/shard_map/bmcn,mnl->blmc/dot_general | solution.py:31
  59.4 1.0 copy.25
  60.4 4.6 %all-to-all-start = ((bf16[64,80,8,2]{1,3,2,0:T(2,128)(2,1)}), bf16[64,80,8,2]{1,3,2,0:T(2,128)(2,1)S(1)}, u32[]{:S(2)}, u32[]{:S(2)}) async-start(bf16[64,80,8,2]{1,3,2,0:T(2,128)(2,1)} %copy.25), calls=%async_computation | async-start | bytes 524288 | tf_op jit(solution)/shard_map/all_to_all | solution.py:34
  65.0 0.0 copy-done.2
  65.0 12.1 %cosine_convert_fusion = (bf16[128,1,5120]{2,0,1:T(8,128)(2,1)S(1)}, bf16[128,1,5120]{2,0,1:T(8,128)(2,1)}) fusion(s32[128]{0:T(128)S(1)} %copy-done.2), kind=kLoop, calls=%fused_computation.11 | loop fusion | flops 7864320 | bytes 2621952 | tf_op jit(solution)/shard_map/convert
  77.1 0.0 all-to-all-done
  77.1 0.2 copy.39
  77.3 4.0 %copy.31 = bf16[4,16,80,8,2]{3,4,0,2,1:T(2,128)(2,1)} copy(bf16[4,16,80,8,2]{2,1,3,4,0:T(8,128)(2,1)S(1)} %bitcast.30) | data formatting | bytes 327680 | tf_op jit(solution)/shard_map/all_to_all | solution.py:34
  81.2 8.6 %reshape.114 = bf16[16,2,2560]{2,1,0:T(2,128)(2,1)} reshape(bf16[1280,4,2,8]{3,2,1,0:T(2,128)(2,1)} %bitcast.26) | data formatting | bytes 327680
  89.8 6.5 %all-to-all-start.1 = ((bf16[16,2,2560]{2,1,0:T(2,128)(2,1)}), bf16[16,2,2560]{2,1,0:T(2,128)(2,1)S(1)}, u32[]{:S(2)}, u32[]{:S(2)}) async-start(bf16[16,2,2560]{2,1,0:T(2,128)(2,1)} %reshape.114), calls=%async_computation.1 | async-start | bytes 327680 | tf_op jit(solution)/shard_map/all_to_all | solution.py:33
  96.4 1.6 %pad_maximum_fusion = bf16[128,2,5120]{2,0,1:T(8,128)(2,1)S(1)} fusion(bf16[128,1,5120]{2,0,1:T(8,128)(2,1)} %get-tuple-element.5, bf16[128,1,5120]{2,0,1:T(8,128)(2,1)S(1)} %get-tuple-element.4), kind=kLoop, calls=%fused_computation.7 | loop fusion | flops 1310720 | bytes 5242880 | tf_op jit(solution)/shard_map/stack | solution.py:14
  97.9 4.2 %copy.29 = bf16[128,2,5120]{2,1,0:T(2,128)(2,1)} copy(bf16[128,2,5120]{2,0,1:T(8,128)(2,1)S(1)} %pad_maximum_fusion) | data formatting | bytes 5242880 | tf_op jit(solution)/shard_map/stack | solution.py:14
  102.1 6.5 %convert_element_type.52 = bf16[256,5120]{1,0:T(8,128)(2,1)} reshape(bf16[128,2,5120]{2,1,0:T(2,128)(2,1)} %copy.29) | data formatting | bytes 5242880 | tf_op jit(solution)/shard_map/convert_element_type | solution.py:15
  108.6 0.0 all-to-all-done.1
  108.6 4.1 %reshape.115 = bf16[1280,4,2,8]{3,2,1,0:T(2,128)(2,1)} reshape(bf16[16,2,2560]{2,1,0:T(2,128)(2,1)S(1)} %all-to-all-done.1) | data formatting | bytes 327680
  112.7 5.2 %copy.28 = bf16[4,16,80,8,2]{2,0,4,3,1:T(4,128)(2,1)S(1)} copy(bf16[4,16,80,8,2]{3,4,0,2,1:T(2,128)(2,1)} %bitcast.27) | data formatting | bytes 327680 | tf_op jit(solution)/shard_map/all_to_all | solution.py:33
  117.9 0.2 reshape.112
  118.1 0.0 copy-start.1
  118.1 3.4 %fusion.1 = f32[320,5120]{1,0:T(8,128)S(1)} fusion(bf16[320,256]{0,1:T(8,128)(2,1)S(1)} %reshape.112, bf16[256,5120]{1,0:T(8,128)(2,1)} %convert_element_type.52), kind=kOutput, calls=%fused_computation.2 | convolution fusion | flops 843776000 | bytes 9338880 | tf_op jit(solution)/shard_map/dot_general | solution.py:43
  121.6 0.0 copy-done.1
  121.6 2.7 %multiply_convert_fusion = bf16[4,80,5120]{2,1,0:T(8,128)(2,1)} fusion(f32[4,80,5120]{2,1,0:T(8,128)S(1)} %bitcast.25, bf16[4,80,5120]{2,1,0:T(8,128)(2,1)S(1)} %copy-done.1), kind=kLoop, calls=%fused_computation.3 | loop fusion | flops 4915200 | bytes 13107200 | tf_op jit(solution)/shard_map/convert_element_type | solution.py:47
Async XLA Ops:
  7.2 49.6 %copy-start = (bf16[8,1280,80]{1,2,0:T(8,128)(2,1)S(1)}, bf16[8,1280,80]{1,2,0:T(8,128)(2,1)}, u32[]{:S(2)}) copy-start(bf16[8,1280,80]{1,2,0:T(8,128)(2,1)} %param.12) | copy-start | bytes 4915204
  7.2 49.6 %all-gather.2.cloned.1.call-start = ((), (), s32[]{:S(2)}) async-start(), calls=%async_computation.2 | async-start | bytes 2785280 | tf_op jit(solution)/shard_map/all_gather | solution.py:30
  12.3 52.7 %copy-start.2 = (s32[128]{0:T(128)S(1)}, s32[128]{0:T(128)}, u32[]{:S(2)}) copy-start(s32[128]{0:T(128)} %param.11) | copy-start | bytes 1540
  60.4 16.7 %all-to-all-start = ((bf16[64,80,8,2]{1,3,2,0:T(2,128)(2,1)}), bf16[64,80,8,2]{1,3,2,0:T(2,128)(2,1)S(1)}, u32[]{:S(2)}, u32[]{:S(2)}) async-start(bf16[64,80,8,2]{1,3,2,0:T(2,128)(2,1)} %copy.25), calls=%async_computation | async-start | bytes 524288 | tf_op jit(solution)/shard_map/all_to_all | solution.py:34
  89.8 18.8 %all-to-all-start.1 = ((bf16[16,2,2560]{2,1,0:T(2,128)(2,1)}), bf16[16,2,2560]{2,1,0:T(2,128)(2,1)S(1)}, u32[]{:S(2)}, u32[]{:S(2)}) async-start(bf16[16,2,2560]{2,1,0:T(2,128)(2,1)} %reshape.114), calls=%async_computation.1 | async-start | bytes 327680 | tf_op jit(solution)/shard_map/all_to_all | solution.py:33
  118.1 3.4 %copy-start.1 = (bf16[4,80,5120]{2,1,0:T(8,128)(2,1)S(1)}, bf16[4,80,5120]{2,1,0:T(8,128)(2,1)}, u32[]{:S(2)}) copy-start(bf16[4,80,5120]{2,1,0:T(8,128)(2,1)} %param.13) | copy-start | bytes 9830404
Sparse Core Ops, SparseCore 0:
  12.4 44.2 all-gather.1
where the time goes:
time: 132 us; the launch traced here: 131 us
  waiting for transfers between devices  44.4 us (34%)
  local copies, waits for them, and re-layouts  35.5 us (27%)
  other arithmetic  19.9 us (15%)
  between operations  14.1 us (11%)
  starting transfers between devices  11.2 us (8%)
  matrix products  6.1 us (5%)
    all_gather x1, waiting for transfers between devices, per_device(): everyone = lax.all_gather(coefficients, 'mem', axis=0, tiled=True)  44.4 us
    unnamed x8, local copies, waits for them, and re-layouts  12.8 us
    another operation x1, other arithmetic  12.1 us
    all_to_all x1, starting transfers between devices, per_device(): lax.all_to_all(lax.all_to_all(fourier, 'mem', split_axis=0, concat_axis=1...  6.53 us
    convert_element_type x1, local copies, waits for them, and re-layouts, basis_table(): stacked.reshape(2 * wavenumber.shape[0], lon_count).astype(jnp.bfloat16)  6.47 us
    all_to_all x1, local copies, waits for them, and re-layouts, per_device(): lax.all_to_all(lax.all_to_all(fourier, 'mem', split_axis=0, concat_axis=1...  5.18 us
    all_to_all x1, starting transfers between devices, per_device(): lax.all_to_all(fourier, 'mem', split_axis=0, concat_axis=1, tiled=True)  4.59 us
    another operation x1, local copies, waits for them, and re-layouts, basis_table(): stacked = jnp.stack([jnp.cos(angles), -jnp.sin(angles)], axis=1)  4.19 us
  transfers between devices with their start and end apart: 3, of which 1 were waited for; matrix products, arithmetic and copies ran while one was open for 19% of the time, Pallas kernels for 0%

commit v1 on v0

--- a/solution.py
+++ b/solution.py
@@ -5,6 +5,12 @@
 from jax.sharding import PartitionSpec as P
 
 clip_level = 0.9
+
+
+def joined_along(blocks, dim):
+    shape = list(blocks.shape[1:])
+    shape[dim] *= blocks.shape[0]
+    return jnp.moveaxis(blocks, 0, dim).reshape(shape)
 
 
 def basis_table(wavenumber, lon_count):
@@ -27,7 +33,19 @@
     )
     new_state = kept_mask[None, None, :, None, :] * updated
     coefficients = jnp.sum(new_state, axis=0).astype(jnp.bfloat16)
-    everyone = lax.all_gather(coefficients, "mem", axis=0, tiled=True)
+    devices = lax.axis_size("mem")
+    pairs = [(i, (i + 1) % devices) for i in range(devices)]
+    back = [(b, a) for a, b in pairs]
+    lower, upper = ([], [])
+    for step in range(devices - 1):
+        if step % 2 == 0:
+            lower.append(lax.ppermute(lower[-1] if lower else coefficients, "mem", pairs))
+        else:
+            upper.append(lax.ppermute(upper[-1] if upper else coefficients, "mem", back))
+    tiles = jnp.stack([*lower[::-1], coefficients, *upper])
+    shift = lax.axis_index("mem") - len(lower)
+    tiles = tiles[(jnp.arange(devices) - shift) % devices]
+    everyone = joined_along(tiles, 0)
     product = jnp.einsum("bmcn,mnl->blmc", everyone, tables, preferred_element_type=jnp.float32)
     fourier = product.astype(jnp.bfloat16)
     banded = lax.all_to_all(

time: 132 us -> 144 us (1.091)
  starting transfers between devices: 11.2 us -> 55.6 us
  waiting for transfers between devices: 44.4 us -> 9.39 us
  local copies, waits for them, and re-layouts: 35.5 us -> 51.4 us
  between operations: 14.1 us -> 0.75 us
    all_gather x1 -> x0, waiting for transfers between devices: 44.4 us -> none  [per_device(): everyone = lax.all_gather(coefficients, 'mem', axis=0, tiled=True)]
    ppermute x0 -> x15, starting transfers between devices: none -> 37.6 us  [the longest x7 29.7 us: per_device(): lax.ppermute(upper[-1] if upper else coefficients, 'mem', back)]
    unnamed x8 -> x23, local copies, waits for them, and re-layouts: 12.8 us -> 24.8 us
    ppermute x0 -> x15, waiting for transfers between devices: none -> 9.38 us  [the longest x8 9.07 us: per_device(): lax.ppermute(lower[-1] if lower else coefficients, 'mem', pairs)]
    all_to_all x1, starting transfers between devices: 4.59 us -> 11.2 us  [per_device(): lax.all_to_all(fourier, 'mem', split_axis=0, concat_axis=1, tiled=True)]
    gather x0 -> x1, local copies, waits for them, and re-layouts: none -> 3.95 us  [per_device(): tiles = tiles[(jnp.arange(devices) - shift) % devices]]
  transfers between devices with their start and end apart: 3 -> 17, of which waited for: 1 -> 10; matrix products, arithmetic and copies ran while one was open for 19% -> 25% of each run, Pallas kernels for 0% -> 0%
where the time goes in v1:
time: 144 us; the launch traced here: 143 us
  starting transfers between devices  55.6 us (39%)
  local copies, waits for them, and re-layouts  51.4 us (36%)
  other arithmetic  19.9 us (14%)
  waiting for transfers between devices  9.39 us (7%)
  matrix products  6.11 us (4%)
    ppermute x7, starting transfers between devices, per_device(): lax.ppermute(upper[-1] if upper else coefficients, 'mem', back)  29.7 us
    unnamed x23, local copies, waits for them, and re-layouts  24.8 us
    another operation x1, other arithmetic  12.1 us
    all_to_all x1, starting transfers between devices, per_device(): lax.all_to_all(fourier, 'mem', split_axis=0, concat_axis=1, tiled=True)  11.2 us
    ppermute x8, waiting for transfers between devices, per_device(): lax.ppermute(lower[-1] if lower else coefficients, 'mem', pairs)  9.07 us
    ppermute x8, starting transfers between devices, per_device(): lax.ppermute(lower[-1] if lower else coefficients, 'mem', pairs)  7.95 us
    all_to_all x1, starting transfers between devices, per_device(): lax.all_to_all(lax.all_to_all(fourier, 'mem', split_axis=0, concat_axis=1...  6.76 us
    convert_element_type x1, local copies, waits for them, and re-layouts, basis_table(): stacked.reshape(2 * wavenumber.shape[0], lon_count).astype(jnp.bfloat16)  6.49 us
  transfers between devices with their start and end apart: 17, of which 10 were waited for; matrix products, arithmetic and copies ran while one was open for 25% of the time, Pallas kernels for 0%

profile of v1, /device:TPU:1, one launch (start us, length us, event | category | flops | bytes accessed | tf_op | source)
XLA Modules:
  0.0 143.2 jit_solution(16881253127821123155)
XLA Ops:
  0.6 0.9 dynamic_slice.3
  1.6 3.5 %fusion.23 = (bf16[4,8,2,1280]{3,2,1,0:T(2,128)(2,1)S(1)}, f32[3,4,8,2,1280]{4,3,2,1,0:T(2,128)}) fusion(f32[3,4,8,2,1280]{4,3,2,1,0:T(2,128)} %param.8, f32[3,1280]{1,0:T(4,128)} %param.10, f32[3,4,8,2,1280]{4,3,2,1,0:T(2,128)} %param.7, f32[3]{0:T(128)} %param.9, f32[8,1280]{1,0:T(8,128)S(1)} %fusion.20), kind=kLoop, calls=%fused_computation.48 | loop fusion | flops 1146880 | bytes 3169292 | tf_op jit(solution)/shard_map/reduce_sum | solution.py:35
  5.1 3.0 %collective-permute-start = (bf16[4,8,2,1280]{3,1,2,0:T(8,128)(2,1)S(1)}, bf16[4,8,2,1280]{3,1,2,0:T(8,128)(2,1)S(1)}, u32[]{:S(2)}, u32[]{:S(2)}) collective-permute-start(bf16[4,8,2,1280]{3,1,2,0:T(8,128)(2,1)S(1)} %copy.41), channel_id=1, source_target_pairs={{0,16},{16,32},{32,48},{48,64},{64,80},{80,96},{96,112},{112,128},... | collective-permute-start | bytes 491528 | tf_op jit(solution)/shard_map/ppermute | solution.py:42
  8.1 2.3 %collective-permute-done = bf16[4,8,2,1280]{3,1,2,0:T(8,128)(2,1)S(1)} collective-permute-done((bf16[4,8,2,1280]{3,1,2,0:T(8,128)(2,1)S(1)}, bf16[4,8,2,1280]{3,1,2,0:T(8,128)(2,1)S(1)}, u32[]{:S(2)}, u32[]{:S(2)}) %collective-permute-start) | collective-permute-done | bytes 163872 | tf_op jit(solution)/shard_map/ppermute | solution.py:42
  10.4 2.5 %collective-permute-start.1 = (bf16[4,8,2,1280]{3,1,2,0:T(8,128)(2,1)S(1)}, bf16[4,8,2,1280]{3,1,2,0:T(8,128)(2,1)S(1)}, u32[]{:S(2)}, u32[]{:S(2)}) collective-permute-start(bf16[4,8,2,1280]{3,1,2,0:T(8,128)(2,1)S(1)} %collective-permute-done), channel_id=1, source_target_pairs={{0,16},{16,32},{32,48},{48,64},{64,80},{80,96},{96,112},{112,128},... | collective-permute-start | bytes 491528 | tf_op jit(solution)/shard_map/ppermute | solution.py:42
  12.8 2.0 %collective-permute-start.8 = (bf16[4,8,2,1280]{3,1,2,0:T(8,128)(2,1)S(1)}, bf16[4,8,2,1280]{3,1,2,0:T(8,128)(2,1)S(1)}, u32[]{:S(2)}, u32[]{:S(2)}) collective-permute-start(bf16[4,8,2,1280]{3,1,2,0:T(8,128)(2,1)S(1)} %copy.41), channel_id=1, source_target_pairs={{16,0},{32,16},{48,32},{64,48},{80,64},{96,80},{112,96},{128,112},... | collective-permute-start | bytes 491528 | tf_op jit(solution)/shard_map/ppermute | solution.py:44
  14.9 0.9 collective-permute-done.1
  15.8 1.8 %collective-permute-start.2 = (bf16[4,8,2,1280]{3,1,2,0:T(8,128)(2,1)S(1)}, bf16[4,8,2,1280]{3,1,2,0:T(8,128)(2,1)S(1)}, u32[]{:S(2)}, u32[]{:S(2)}) collective-permute-start(bf16[4,8,2,1280]{3,1,2,0:T(8,128)(2,1)S(1)} %collective-permute-done.1), channel_id=1, source_target_pairs={{0,16},{16,32},{32,48},{48,64},{64,80},{80,96},{96,112},{112,128},... | collective-permute-start | bytes 491528 | tf_op jit(solution)/shard_map/ppermute | solution.py:42
  17.6 3.2 %collective-permute-start.9 = (bf16[4,8,2,1280]{3,1,2,0:T(8,128)(2,1)S(1)}, bf16[4,8,2,1280]{3,1,2,0:T(8,128)(2,1)S(1)}, u32[]{:S(2)}, u32[]{:S(2)}) collective-permute-start(bf16[4,8,2,1280]{3,1,2,0:T(8,128)(2,1)S(1)} %collective-permute-done.8), channel_id=1, source_target_pairs={{16,0},{32,16},{48,32},{64,48},{80,64},{96,80},{112,96},{128,112},... | collective-permute-start | bytes 491528 | tf_op jit(solution)/shard_map/ppermute | solution.py:44
  20.8 0.9 collective-permute-done.2
  22.3 4.5 %collective-permute-start.10 = (bf16[4,8,2,1280]{3,1,2,0:T(8,128)(2,1)S(1)}, bf16[4,8,2,1280]{3,1,2,0:T(8,128)(2,1)S(1)}, u32[]{:S(2)}, u32[]{:S(2)}) collective-permute-start(bf16[4,8,2,1280]{3,1,2,0:T(8,128)(2,1)S(1)} %collective-permute-done.9), channel_id=1, source_target_pairs={{16,0},{32,16},{48,32},{64,48},{80,64},{96,80},{112,96},{128,112},... | collective-permute-start | bytes 491528 | tf_op jit(solution)/shard_map/ppermute | solution.py:44
  26.8 0.9 collective-permute-done.3
  27.8 4.9 %collective-permute-start.11 = (bf16[4,8,2,1280]{3,1,2,0:T(8,128)(2,1)S(1)}, bf16[4,8,2,1280]{3,1,2,0:T(8,128)(2,1)S(1)}, u32[]{:S(2)}, u32[]{:S(2)}) collective-permute-start(bf16[4,8,2,1280]{3,1,2,0:T(8,128)(2,1)S(1)} %collective-permute-done.10), channel_id=1, source_target_pairs={{16,0},{32,16},{48,32},{64,48},{80,64},{96,80},{112,96},{128,112},... | collective-permute-start | bytes 491528 | tf_op jit(solution)/shard_map/ppermute | solution.py:44
  32.7 0.9 collective-permute-done.4
  33.8 4.9 %collective-permute-start.12 = (bf16[4,8,2,1280]{3,1,2,0:T(8,128)(2,1)S(1)}, bf16[4,8,2,1280]{3,1,2,0:T(8,128)(2,1)S(1)}, u32[]{:S(2)}, u32[]{:S(2)}) collective-permute-start(bf16[4,8,2,1280]{3,1,2,0:T(8,128)(2,1)S(1)} %collective-permute-done.11), channel_id=1, source_target_pairs={{16,0},{32,16},{48,32},{64,48},{80,64},{96,80},{112,96},{128,112},... | collective-permute-start | bytes 491528 | tf_op jit(solution)/shard_map/ppermute | solution.py:44
  38.7 1.0 collective-permute-done.5
  39.7 5.0 %collective-permute-start.13 = (bf16[4,8,2,1280]{3,1,2,0:T(8,128)(2,1)S(1)}, bf16[4,8,2,1280]{3,1,2,0:T(8,128)(2,1)S(1)}, u32[]{:S(2)}, u32[]{:S(2)}) collective-permute-start(bf16[4,8,2,1280]{3,1,2,0:T(8,128)(2,1)S(1)} %collective-permute-done.12), channel_id=1, source_target_pairs={{16,0},{32,16},{48,32},{64,48},{80,64},{96,80},{112,96},{128,112},... | collective-permute-start | bytes 491528 | tf_op jit(solution)/shard_map/ppermute | solution.py:44
  44.8 1.2 collective-permute-done.6
  46.0 5.1 %collective-permute-start.14 = (bf16[4,8,2,1280]{3,1,2,0:T(8,128)(2,1)S(1)}, bf16[4,8,2,1280]{3,1,2,0:T(8,128)(2,1)S(1)}, u32[]{:S(2)}, u32[]{:S(2)}) collective-permute-start(bf16[4,8,2,1280]{3,1,2,0:T(8,128)(2,1)S(1)} %collective-permute-done.13), channel_id=1, source_target_pairs={{16,0},{32,16},{48,32},{64,48},{80,64},{96,80},{112,96},{128,112},... | collective-permute-start | bytes 491528 | tf_op jit(solution)/shard_map/ppermute | solution.py:44
  51.1 1.0 collective-permute-done.7
  52.1 0.7 bitcast_dynamic-update-slice_fusion.15
  52.8 1.6 %bitcast_dynamic-update-slice_fusion.14 = bf16[16,4,8,2,1280]{4,2,3,1,0:T(8,128)(2,1)} fusion(bf16[16,4,8,2,1280]{4,2,3,1,0:T(8,128)(2,1)} %bitcast_dynamic-update-slice_fusion.15, bf16[4,8,2,1280]{3,1,2,0:T(8,128)(2,1)} %collective-permute-done.6), kind=kLoop, calls=%fused_computation.37 | loop fusion | bytes 327680
  54.4 1.6 %bitcast_dynamic-update-slice_fusion.13 = bf16[16,4,8,2,1280]{4,2,3,1,0:T(8,128)(2,1)} fusion(bf16[16,4,8,2,1280]{4,2,3,1,0:T(8,128)(2,1)} %bitcast_dynamic-update-slice_fusion.14, bf16[4,8,2,1280]{3,1,2,0:T(8,128)(2,1)} %collective-permute-done.5), kind=kLoop, calls=%fused_computation.36 | loop fusion | bytes 327680
  56.0 0.7 bitcast_dynamic-update-slice_fusion.12
  56.7 0.7 bitcast_dynamic-update-slice_fusion.11
  57.3 0.7 bitcast_dynamic-update-slice_fusion.10
  58.0 0.7 bitcast_dynamic-update-slice_fusion.9
  58.7 0.7 bitcast_dynamic-update-slice_fusion.8
  59.4 0.7 bitcast_dynamic-update-slice_fusion.7
  60.1 0.7 bitcast_dynamic-update-slice_fusion.6
  60.7 0.7 bitcast_dynamic-update-slice_fusion.5
  61.4 0.7 bitcast_dynamic-update-slice_fusion.4
  64.1 0.7 bitcast_dynamic-update-slice_fusion
  64.8 3.9 %gather_fusion = bf16[16,4,8,2,1280]{4,2,3,1,0:T(8,128)(2,1)} fusion(bf16[16,4,8,2,1280]{4,2,3,1,0:T(8,128)(2,1)} %bitcast_dynamic-update-slice_fusion, s32[1024]{0:T(1024)S(1)} %pad_clamp_fusion), kind=kCustom, calls=%fused_computation | custom fusion | bytes 5242944 | tf_op jit(solution)/shard_map/gather | solution.py:47
  68.8 2.7 %fusion.15 = bf16[64,80,8,2]{1,0,3,2:T(8,128)(2,1)S(1)} fusion(bf16[8,1280,80]{1,2,0:T(8,128)(2,1)S(1)} %copy-done, bf16[64,8,2,1280]{3,1,2,0:T(8,128)(2,1)} %bitcast.63), kind=kOutput, calls=%fused_computation.19 | convolution fusion | flops 209797120 | bytes 4423680 | tf_op jit(solution)/shard_map/bmcn,mnl->blmc/dot_general | solution.py:49
  71.5 1.0 copy.26
  72.4 11.2 %all-to-all-start = ((bf16[64,80,8,2]{1,3,2,0:T(2,128)(2,1)}), bf16[64,80,8,2]{1,3,2,0:T(2,128)(2,1)S(1)}, u32[]{:S(2)}, u32[]{:S(2)}) async-start(bf16[64,80,8,2]{1,3,2,0:T(2,128)(2,1)} %copy.26), calls=%async_computation | async-start | bytes 524288 | tf_op jit(solution)/shard_map/all_to_all | solution.py:52
  83.6 12.1 %cosine_convert_fusion = (bf16[128,1,5120]{2,0,1:T(8,128)(2,1)S(1)}, bf16[128,1,5120]{2,0,1:T(8,128)(2,1)}) fusion(s32[128]{0:T(128)S(1)} %copy-done.2), kind=kLoop, calls=%fused_computation.12 | loop fusion | flops 7864320 | bytes 2621952 | tf_op jit(solution)/shard_map/convert
  95.9 4.0 %copy.32 = bf16[4,16,80,8,2]{3,4,0,2,1:T(2,128)(2,1)} copy(bf16[4,16,80,8,2]{2,1,3,4,0:T(8,128)(2,1)S(1)} %bitcast.66) | data formatting | bytes 327680 | tf_op jit(solution)/shard_map/all_to_all | solution.py:52
  99.8 8.6 %reshape.183 = bf16[16,2,2560]{2,1,0:T(2,128)(2,1)} reshape(bf16[1280,4,2,8]{3,2,1,0:T(2,128)(2,1)} %bitcast.61) | data formatting | bytes 327680
  108.5 6.8 %all-to-all-start.1 = ((bf16[16,2,2560]{2,1,0:T(2,128)(2,1)}), bf16[16,2,2560]{2,1,0:T(2,128)(2,1)S(1)}, u32[]{:S(2)}, u32[]{:S(2)}) async-start(bf16[16,2,2560]{2,1,0:T(2,128)(2,1)} %reshape.183), calls=%async_computation.1 | async-start | bytes 327680 | tf_op jit(solution)/shard_map/all_to_all | solution.py:51
  115.2 1.6 %pad_maximum_fusion = bf16[128,2,5120]{2,0,1:T(8,128)(2,1)S(1)} fusion(bf16[128,1,5120]{2,0,1:T(8,128)(2,1)} %get-tuple-element.5, bf16[128,1,5120]{2,0,1:T(8,128)(2,1)S(1)} %get-tuple-element.4), kind=kLoop, calls=%fused_computation.8 | loop fusion | flops 1310720 | bytes 5242880 | tf_op jit(solution)/shard_map/stack | solution.py:20
  116.8 4.2 %copy.30 = bf16[128,2,5120]{2,1,0:T(2,128)(2,1)} copy(bf16[128,2,5120]{2,0,1:T(8,128)(2,1)S(1)} %pad_maximum_fusion) | data formatting | bytes 5242880 | tf_op jit(solution)/shard_map/stack | solution.py:20
  121.0 6.5 %convert_element_type.63 = bf16[256,5120]{1,0:T(8,128)(2,1)} reshape(bf16[128,2,5120]{2,1,0:T(2,128)(2,1)} %copy.30) | data formatting | bytes 5242880 | tf_op jit(solution)/shard_map/convert_element_type | solution.py:21
  127.5 4.1 %reshape.184 = bf16[1280,4,2,8]{3,2,1,0:T(2,128)(2,1)} reshape(bf16[16,2,2560]{2,1,0:T(2,128)(2,1)S(1)} %all-to-all-done.1) | data formatting | bytes 327680
  131.6 5.2 %copy.29 = bf16[4,16,80,8,2]{2,0,4,3,1:T(4,128)(2,1)S(1)} copy(bf16[4,16,80,8,2]{3,4,0,2,1:T(2,128)(2,1)} %bitcast.62) | data formatting | bytes 327680 | tf_op jit(solution)/shard_map/all_to_all | solution.py:51
  137.0 3.4 %fusion.1 = f32[320,5120]{1,0:T(8,128)S(1)} fusion(bf16[320,256]{0,1:T(8,128)(2,1)S(1)} %reshape.173, bf16[256,5120]{1,0:T(8,128)(2,1)} %convert_element_type.63), kind=kOutput, calls=%fused_computation.3 | convolution fusion | flops 843776000 | bytes 9338880 | tf_op jit(solution)/shard_map/dot_general | solution.py:61
  140.4 2.7 %multiply_convert_fusion = bf16[4,80,5120]{2,1,0:T(8,128)(2,1)} fusion(f32[4,80,5120]{2,1,0:T(8,128)S(1)} %bitcast.60, bf16[4,80,5120]{2,1,0:T(8,128)(2,1)S(1)} %copy-done.1), kind=kLoop, calls=%fused_computation.4 | loop fusion | flops 4915200 | bytes 13107200 | tf_op jit(solution)/shard_map/convert_element_type | solution.py:65
  (29 shorter events, 3.5 us)
Async XLA Ops:
  0.6 68.1 %copy-start = (bf16[8,1280,80]{1,2,0:T(8,128)(2,1)S(1)}, bf16[8,1280,80]{1,2,0:T(8,128)(2,1)}, u32[]{:S(2)}) copy-start(bf16[8,1280,80]{1,2,0:T(8,128)(2,1)} %param.12) | copy-start | bytes 4915204
  5.1 5.3 %collective-permute-start = (bf16[4,8,2,1280]{3,1,2,0:T(8,128)(2,1)S(1)}, bf16[4,8,2,1280]{3,1,2,0:T(8,128)(2,1)S(1)}, u32[]{:S(2)}, u32[]{:S(2)}) collective-permute-start(bf16[4,8,2,1280]{3,1,2,0:T(8,128)(2,1)S(1)} %copy.41), channel_id=1, source_target_pairs={{0,16},{16,32},{32,48},{48,64},{64,80},{80,96},{96,112},{112,128},... | collective-permute-start | bytes 491528 | tf_op jit(solution)/shard_map/ppermute | solution.py:42
  10.4 5.4 %collective-permute-start.1 = (bf16[4,8,2,1280]{3,1,2,0:T(8,128)(2,1)S(1)}, bf16[4,8,2,1280]{3,1,2,0:T(8,128)(2,1)S(1)}, u32[]{:S(2)}, u32[]{:S(2)}) collective-permute-start(bf16[4,8,2,1280]{3,1,2,0:T(8,128)(2,1)S(1)} %collective-permute-done), channel_id=1, source_target_pairs={{0,16},{16,32},{32,48},{48,64},{64,80},{80,96},{96,112},{112,128},... | collective-permute-start | bytes 491528 | tf_op jit(solution)/shard_map/ppermute | solution.py:42
  12.8 4.7 %collective-permute-start.8 = (bf16[4,8,2,1280]{3,1,2,0:T(8,128)(2,1)S(1)}, bf16[4,8,2,1280]{3,1,2,0:T(8,128)(2,1)S(1)}, u32[]{:S(2)}, u32[]{:S(2)}) collective-permute-start(bf16[4,8,2,1280]{3,1,2,0:T(8,128)(2,1)S(1)} %copy.41), channel_id=1, source_target_pairs={{16,0},{32,16},{48,32},{64,48},{80,64},{96,80},{112,96},{128,112},... | collective-permute-start | bytes 491528 | tf_op jit(solution)/shard_map/ppermute | solution.py:44
  15.8 6.0 %collective-permute-start.2 = (bf16[4,8,2,1280]{3,1,2,0:T(8,128)(2,1)S(1)}, bf16[4,8,2,1280]{3,1,2,0:T(8,128)(2,1)S(1)}, u32[]{:S(2)}, u32[]{:S(2)}) collective-permute-start(bf16[4,8,2,1280]{3,1,2,0:T(8,128)(2,1)S(1)} %collective-permute-done.1), channel_id=1, source_target_pairs={{0,16},{16,32},{32,48},{48,64},{64,80},{80,96},{96,112},{112,128},... | collective-permute-start | bytes 491528 | tf_op jit(solution)/shard_map/ppermute | solution.py:42
  17.6 4.7 %collective-permute-start.9 = (bf16[4,8,2,1280]{3,1,2,0:T(8,128)(2,1)S(1)}, bf16[4,8,2,1280]{3,1,2,0:T(8,128)(2,1)S(1)}, u32[]{:S(2)}, u32[]{:S(2)}) collective-permute-start(bf16[4,8,2,1280]{3,1,2,0:T(8,128)(2,1)S(1)} %collective-permute-done.8), channel_id=1, source_target_pairs={{16,0},{32,16},{48,32},{64,48},{80,64},{96,80},{112,96},{128,112},... | collective-permute-start | bytes 491528 | tf_op jit(solution)/shard_map/ppermute | solution.py:44
  21.7 6.0 %collective-permute-start.3 = (bf16[4,8,2,1280]{3,1,2,0:T(8,128)(2,1)S(1)}, bf16[4,8,2,1280]{3,1,2,0:T(8,128)(2,1)S(1)}, u32[]{:S(2)}, u32[]{:S(2)}) collective-permute-start(bf16[4,8,2,1280]{3,1,2,0:T(8,128)(2,1)S(1)} %collective-permute-done.2), channel_id=1, source_target_pairs={{0,16},{16,32},{32,48},{48,64},{64,80},{80,96},{96,112},{112,128},... | collective-permute-start | bytes 491528 | tf_op jit(solution)/shard_map/ppermute | solution.py:42
  22.3 5.5 %collective-permute-start.10 = (bf16[4,8,2,1280]{3,1,2,0:T(8,128)(2,1)S(1)}, bf16[4,8,2,1280]{3,1,2,0:T(8,128)(2,1)S(1)}, u32[]{:S(2)}, u32[]{:S(2)}) collective-permute-start(bf16[4,8,2,1280]{3,1,2,0:T(8,128)(2,1)S(1)} %collective-permute-done.9), channel_id=1, source_target_pairs={{16,0},{32,16},{48,32},{64,48},{80,64},{96,80},{112,96},{128,112},... | collective-permute-start | bytes 491528 | tf_op jit(solution)/shard_map/ppermute | solution.py:44
  27.7 6.0 %collective-permute-start.4 = (bf16[4,8,2,1280]{3,1,2,0:T(8,128)(2,1)S(1)}, bf16[4,8,2,1280]{3,1,2,0:T(8,128)(2,1)S(1)}, u32[]{:S(2)}, u32[]{:S(2)}) collective-permute-start(bf16[4,8,2,1280]{3,1,2,0:T(8,128)(2,1)S(1)} %collective-permute-done.3), channel_id=1, source_target_pairs={{0,16},{16,32},{32,48},{48,64},{64,80},{80,96},{96,112},{112,128},... | collective-permute-start | bytes 491528 | tf_op jit(solution)/shard_map/ppermute | solution.py:42
  27.8 6.0 %collective-permute-start.11 = (bf16[4,8,2,1280]{3,1,2,0:T(8,128)(2,1)S(1)}, bf16[4,8,2,1280]{3,1,2,0:T(8,128)(2,1)S(1)}, u32[]{:S(2)}, u32[]{:S(2)}) collective-permute-start(bf16[4,8,2,1280]{3,1,2,0:T(8,128)(2,1)S(1)} %collective-permute-done.10), channel_id=1, source_target_pairs={{16,0},{32,16},{48,32},{64,48},{80,64},{96,80},{112,96},{128,112},... | collective-permute-start | bytes 491528 | tf_op jit(solution)/shard_map/ppermute | solution.py:44
  33.6 6.1 %collective-permute-start.5 = (bf16[4,8,2,1280]{3,1,2,0:T(8,128)(2,1)S(1)}, bf16[4,8,2,1280]{3,1,2,0:T(8,128)(2,1)}, u32[]{:S(2)}, u32[]{:S(2)}) collective-permute-start(bf16[4,8,2,1280]{3,1,2,0:T(8,128)(2,1)S(1)} %collective-permute-done.4), channel_id=1, source_target_pairs={{0,16},{16,32},{32,48},{48,64},{64,80},{80,96},{96,112},{112,128},... | collective-permute-start | bytes 491528 | tf_op jit(solution)/shard_map/ppermute | solution.py:42
  33.8 6.0 %collective-permute-start.12 = (bf16[4,8,2,1280]{3,1,2,0:T(8,128)(2,1)S(1)}, bf16[4,8,2,1280]{3,1,2,0:T(8,128)(2,1)S(1)}, u32[]{:S(2)}, u32[]{:S(2)}) collective-permute-start(bf16[4,8,2,1280]{3,1,2,0:T(8,128)(2,1)S(1)} %collective-permute-done.11), channel_id=1, source_target_pairs={{16,0},{32,16},{48,32},{64,48},{80,64},{96,80},{112,96},{128,112},... | collective-permute-start | bytes 491528 | tf_op jit(solution)/shard_map/ppermute | solution.py:44
  39.7 6.3 %collective-permute-start.6 = (bf16[4,8,2,1280]{3,1,2,0:T(8,128)(2,1)}, bf16[4,8,2,1280]{3,1,2,0:T(8,128)(2,1)}, u32[]{:S(2)}, u32[]{:S(2)}) collective-permute-start(bf16[4,8,2,1280]{3,1,2,0:T(8,128)(2,1)} %collective-permute-done.5), channel_id=1, source_target_pairs={{0,16},{16,32},{32,48},{48,64},{64,80},{80,96},{96,112},{112,128},... | collective-permute-start | bytes 491528 | tf_op jit(solution)/shard_map/ppermute | solution.py:42
  39.7 6.3 %collective-permute-start.13 = (bf16[4,8,2,1280]{3,1,2,0:T(8,128)(2,1)S(1)}, bf16[4,8,2,1280]{3,1,2,0:T(8,128)(2,1)S(1)}, u32[]{:S(2)}, u32[]{:S(2)}) collective-permute-start(bf16[4,8,2,1280]{3,1,2,0:T(8,128)(2,1)S(1)} %collective-permute-done.12), channel_id=1, source_target_pairs={{16,0},{32,16},{48,32},{64,48},{80,64},{96,80},{112,96},{128,112},... | collective-permute-start | bytes 491528 | tf_op jit(solution)/shard_map/ppermute | solution.py:44
  46.0 6.1 %collective-permute-start.7 = (bf16[4,8,2,1280]{3,1,2,0:T(8,128)(2,1)}, bf16[4,8,2,1280]{3,1,2,0:T(8,128)(2,1)S(1)}, u32[]{:S(2)}, u32[]{:S(2)}) collective-permute-start(bf16[4,8,2,1280]{3,1,2,0:T(8,128)(2,1)} %collective-permute-done.6), channel_id=1, source_target_pairs={{0,16},{16,32},{32,48},{48,64},{64,80},{80,96},{96,112},{112,128},... | collective-permute-start | bytes 491528 | tf_op jit(solution)/shard_map/ppermute | solution.py:42
  46.0 18.1 %collective-permute-start.14 = (bf16[4,8,2,1280]{3,1,2,0:T(8,128)(2,1)S(1)}, bf16[4,8,2,1280]{3,1,2,0:T(8,128)(2,1)S(1)}, u32[]{:S(2)}, u32[]{:S(2)}) collective-permute-start(bf16[4,8,2,1280]{3,1,2,0:T(8,128)(2,1)S(1)} %collective-permute-done.13), channel_id=1, source_target_pairs={{16,0},{32,16},{48,32},{64,48},{80,64},{96,80},{112,96},{128,112},... | collective-permute-start | bytes 491528 | tf_op jit(solution)/shard_map/ppermute | solution.py:44
  68.8 14.9 %copy-start.2 = (s32[128]{0:T(128)S(1)}, s32[128]{0:T(128)}, u32[]{:S(2)}) copy-start(s32[128]{0:T(128)} %param.11) | copy-start | bytes 1540
  72.4 23.3 %all-to-all-start = ((bf16[64,80,8,2]{1,3,2,0:T(2,128)(2,1)}), bf16[64,80,8,2]{1,3,2,0:T(2,128)(2,1)S(1)}, u32[]{:S(2)}, u32[]{:S(2)}) async-start(bf16[64,80,8,2]{1,3,2,0:T(2,128)(2,1)} %copy.26), calls=%async_computation | async-start | bytes 524288 | tf_op jit(solution)/shard_map/all_to_all | solution.py:52
  108.5 19.0 %all-to-all-start.1 = ((bf16[16,2,2560]{2,1,0:T(2,128)(2,1)}), bf16[16,2,2560]{2,1,0:T(2,128)(2,1)S(1)}, u32[]{:S(2)}, u32[]{:S(2)}) async-start(bf16[16,2,2560]{2,1,0:T(2,128)(2,1)} %reshape.183), calls=%async_computation.1 | async-start | bytes 327680 | tf_op jit(solution)/shard_map/all_to_all | solution.py:51
  137.0 3.4 %copy-start.1 = (bf16[4,80,5120]{2,1,0:T(8,128)(2,1)S(1)}, bf16[4,80,5120]{2,1,0:T(8,128)(2,1)}, u32[]{:S(2)}) copy-start(bf16[4,80,5120]{2,1,0:T(8,128)(2,1)} %param.13) | copy-start | bytes 9830404
